TPU v7x, 32 devices: a whole 2x2x4 slice. The times are simulated.
32 devices in a mesh: row: 4 (over z), col: 8 (over y, x, core).
Axes of the slice: x: 2, y: 2, z: 4, core: 2. Of those that a mesh axis runs over, the one named last changes fastest.
Arguments:
- node_feats: bfloat16 [4096, 512], P(('row', 'col')), may hold values from -80 to 80
- block_mask: int32 [32, 32], replicated, may hold values from 0 to 1, as said below
- w_qkv: bfloat16 [2, 512, 1536], replicated, may hold values from -0.25 to 0.25
- w_out: bfloat16 [2, 512, 512], replicated, may hold values from -0.79296875 to 0.79296875
- w_up: bfloat16 [2, 512, 1024], replicated, may hold values from -0.25 to 0.25
- w_down: bfloat16 [2, 1024, 512], replicated, may hold values from -0.1875 to 0.1875
- ln_gain: float32 [2, 2, 512], replicated, may hold values from 0.1 to 1.9
- ln_bias: float32 [2, 2, 512], replicated, may hold values from -3 to 3
Outputs:
- nodes_out: bfloat16 [4096, 512], P(('row', 'col'))
Inputs may be any that keep to these rules, and one draw needn't show every extreme that they name: `block_mask`: A symmetric 0/1 table over the 32 node blocks; every block is linked with itself.
All inputs are finite; a program needn't handle non-finite values.
Results may differ from a plain program's by a relative error of at most 0.022.
Values may be sent and summed in bfloat16 or wider, within the bound.
A program may use at most 128 MiB of HBM per device.

v0:
```python
import jax
import jax.numpy as jnp
from jax import lax
from jax.sharding import PartitionSpec as P

HEADS = 8
BLOCK = 128
LAYERS = 2


def combined_all(x, axis, combine):
    everything = jax.tree.map(
        lambda part, kind: lax.all_gather(part.astype(kind), axis),
        x,
        (jnp.bfloat16, jnp.bfloat16, jnp.bfloat16),
    )

    def take(k):
        return jax.tree.map(lambda part, own: part[k].astype(own.dtype), everything, x)

    return lax.fori_loop(
        1, lax.axis_size(axis), lambda k, so_far: combine(so_far, take(k)), take(0)
    )


def layer_norm(values, gain, bias):
    center = values - jnp.mean(values, axis=-1, keepdims=True)
    spread = jnp.mean(center * center, axis=-1, keepdims=True)
    return center * lax.rsqrt(spread + 1e-05) * gain + bias


def per_head(summed, factor):
    count = summed.shape[0]
    return (summed.reshape(count, factor.shape[1], -1) * factor[:, :, None]).reshape(summed.shape)


def combine(first, second):
    sum_a, peak_a, mass_a = first
    sum_b, peak_b, mass_b = second
    peak = jnp.maximum(peak_a, peak_b)
    scale_a = jnp.exp(peak_a - peak)
    scale_b = jnp.exp(peak_b - peak)
    return (
        per_head(sum_a, scale_a) + per_head(sum_b, scale_b),
        peak,
        mass_a * scale_a + mass_b * scale_b,
    )


def partial_attention(queries, keys, values, sub_mask, heads):
    qrows, width = queries.shape
    head_dim = width // heads
    qblock = min(512, qrows)
    nblocks = qrows // qblock
    qsplit = queries.reshape(nblocks, qblock, heads, head_dim)
    ksplit = keys.reshape(-1, heads, head_dim)
    vsplit = values.reshape(-1, heads, head_dim)
    mask_rows = sub_mask.reshape(nblocks, qblock // BLOCK, -1)

    def one_block(item):
        qpart, mpart = item
        scores = jnp.einsum("qhd,khd->hqk", qpart, ksplit, preferred_element_type=jnp.float32) * (
            1.0 / head_dim**0.5
        )
        allowed = (jnp.repeat(jnp.repeat(mpart, BLOCK, axis=0), BLOCK, axis=1) > 0)[None]
        peak = jnp.max(jnp.where(allowed, scores, -1e30), axis=-1, keepdims=True)
        weights = jnp.where(allowed, jnp.exp(scores - peak), 0.0)
        mass = jnp.sum(weights, axis=-1)
        summed = jnp.einsum(
            "hqk,khd->qhd", weights.astype(jnp.bfloat16), vsplit, preferred_element_type=jnp.float32
        )
        return (summed.reshape(qblock, width), peak[:, :, 0].T, mass.T)

    summed, peak, mass = lax.map(one_block, (qsplit, mask_rows))
    return (summed.reshape(qrows, width), peak.reshape(qrows, heads), mass.reshape(qrows, heads))


def per_device(node_feats, block_mask, w_qkv, w_out, w_up, w_down, ln_gain, ln_bias):
    rows, width = node_feats.shape
    heads = HEADS
    n_col = lax.axis_size("col")
    n_row = lax.axis_size("row")
    row_index = lax.axis_index("row")
    col_index = lax.axis_index("col")
    blk_dev = rows // BLOCK
    group_ids = row_index * (n_col * blk_dev) + jnp.arange(n_col * blk_dev, dtype=jnp.int32)
    column_ids = (
        (jnp.arange(n_row, dtype=jnp.int32)[:, None] * n_col + col_index) * blk_dev
        + jnp.arange(blk_dev, dtype=jnp.int32)[None, :]
    ).reshape(-1)
    query_ids, key_ids, own_start = (column_ids, group_ids, row_index * rows)
    sub_mask = jnp.take(jnp.take(block_mask, query_ids, axis=0), key_ids, axis=1)
    x = node_feats
    for layer in range(LAYERS):
        weights = w_qkv[layer]
        qkv = jnp.dot(x, weights, preferred_element_type=jnp.float32).astype(jnp.bfloat16)
        own_q = qkv[:, :width]
        pair = (qkv[:, width : 2 * width], qkv[:, 2 * width :])
        keys, values = (
            lax.all_gather(pair[0], "col", axis=0, tiled=True),
            lax.all_gather(pair[1], "col", axis=0, tiled=True),
        )
        queries = lax.all_gather(own_q, "row", axis=0, tiled=True)
        summed, peak, mass = partial_attention(queries, keys, values, sub_mask, heads)
        summed, peak, mass = combined_all((summed, peak, mass), "row", combine)
        summed = lax.dynamic_slice_in_dim(summed, own_start, rows, 0)
        mass = lax.dynamic_slice_in_dim(mass, own_start, rows, 0)
        attn = per_head(summed, 1.0 / mass).astype(jnp.bfloat16)
        mixed = jnp.dot(attn, w_out[layer], preferred_element_type=jnp.float32)
        hidden = layer_norm(
            x.astype(jnp.float32) + mixed, ln_gain[layer, 0], ln_bias[layer, 0]
        ).astype(jnp.bfloat16)
        up = jax.nn.gelu(jnp.dot(hidden, w_up[layer], preferred_element_type=jnp.float32)).astype(
            jnp.bfloat16
        )
        down = jnp.dot(up, w_down[layer], preferred_element_type=jnp.float32)
        x = layer_norm(
            hidden.astype(jnp.float32) + down, ln_gain[layer, 1], ln_bias[layer, 1]
        ).astype(jnp.bfloat16)
    return x


def solution(mesh):
    placed = (P(("row", "col"), None), P(), P(), P(), P(), P(), P(), P())
    return jax.shard_map(
        per_device, mesh=mesh, in_specs=placed, out_specs=P(("row", "col"), None), check_vma=False
    )
```

profile of v0, /device:TPU:1, one launch (start us, length us, event | category | flops | bytes accessed | tf_op | source)
XLA Modules:
  0.0 254.3 jit_solution(7514067950112595281)
XLA Ops:
  6.5 1.9 convolution_convert_fusion.1
  8.4 0.7 fusion.114
  9.2 0.7 all-gather.11.cloned.1.call-update
  10.0 0.6 gather_fusion
  10.8 0.6 gather_fusion.1
  11.5 1.6 broadcast_in_dim.118
  13.4 15.3 %all_gather.43 = bf16[512,512]{1,0:T(8,128)(2,1)S(1)} all-gather(bf16[128,512]{1,0:T(8,128)(2,1)S(1)} %get-tuple-element.465), channel_id=1, replica_groups=mesh['row'=4,'col'=8] {'row'}, dimensions={0}, use_global_device_ids=true | all-gather | bytes 655360 | tf_op jit(solution)/shard_map/all_gather | solution.py:103
  29.0 6.2 %all-gather.13.cloned.1.call-done = bf16[1024,512]{1,0:T(8,128)(2,1)} async-done(((bf16[128,512]{1,0:T(8,128)(2,1)}), bf16[1024,512]{1,0:T(8,128)(2,1)}) %all-gather.13.cloned.1.call-update) | async-done | bytes 1048592 | tf_op jit(solution)/shard_map/all_gather | solution.py:100
  35.2 1.5 copy.33
  36.6 7.4 %select_reduce_fusion.1 = (f32[8,512]{1,0:T(8,128)S(1)}, f32[8,512,1024]{2,1,0:T(8,128)}) fusion(pred[512,1024]{1,0:T(8,128)(4,1)S(1)} %bitcast.172, bf16[512,8,64]{0,2,1:T(8,128)(2,1)S(1)} %bitcast.180, bf16[1024,8,64]{0,2,1:T(8,128)(2,1)S(1)} %bitcast.178), kind=kOutput, calls=%fused_computation.25 | convolution fusion | flops 549449728 | bytes 18890752 | tf_op jit(solution)/shard_map/while/body/eval_jaxpr/qhd,khd->hqk/dot_general | solution.py:62
  44.1 16.4 %all-gather.11.cloned.1.call-done = bf16[1024,512]{1,0:T(8,128)(2,1)} async-done(((bf16[128,512]{1,0:T(8,128)(2,1)}), bf16[1024,512]{1,0:T(8,128)(2,1)}) %all-gather.11.cloned.1.call-update) | async-done | bytes 1048592 | tf_op jit(solution)/shard_map/all_gather | solution.py:101
  60.4 1.5 copy.29
  61.9 7.6 %fusion.20 = bf16[8,64,512]{2,1,0:T(8,128)(2,1)S(1)} fusion(bf16[1024,8,64]{0,2,1:T(8,128)(2,1)S(1)} %bitcast.183, f32[8,512,1024]{2,1,0:T(8,128)} %get-tuple-element.476, f32[8,512]{1,0:T(8,128)S(1)} %get-tuple-element.475, pred[512,1024]{1,0:T(8,128)(4,1)S(1)} %bitcast.173), kind=kOutput, calls=%fused_computation.41 | convolution fusion | flops 553910272 | bytes 18890752 | tf_op jit(solution)/shard_map/while/body/eval_jaxpr/hqk,khd->qhd/dot_general | solution.py:69
  69.5 1.0 copy.34
  70.7 8.2 %fusion.6 = bf16[8,512]{1,0:T(8,128)(2,1)S(1)} fusion(f32[8,512,1024]{2,1,0:T(8,128)} %get-tuple-element.476, f32[8,512]{1,0:T(8,128)S(1)} %get-tuple-element.475, pred[512,1024]{1,0:T(8,128)(4,1)S(1)} %bitcast.174), kind=kLoop, calls=%fused_computation.26 | loop fusion | flops 16773120 | bytes 17326080 | tf_op jit(solution)/shard_map/while/body/eval_jaxpr/reduce_sum | solution.py:68
  78.9 11.2 %all-gather.1 = bf16[2048,8]{0,1:T(8,128)(2,1)S(1)} all-gather(bf16[512,8]{0,1:T(8,128)(2,1)S(1)} %bitcast.193), channel_id=3, replica_groups=mesh['row'=4,'col'=8] {'row'}, dimensions={0}, use_global_device_ids=true | all-gather | bytes 40960 | tf_op jit(solution)/shard_map/all_gather | solution.py:13
  90.1 10.9 %all-gather = bf16[2048,8]{0,1:T(8,128)(2,1)S(1)} all-gather(bf16[512,8]{0,1:T(8,128)(2,1)S(1)} %convert_bitcast_fusion.3), channel_id=2, replica_groups=mesh['row'=4,'col'=8] {'row'}, dimensions={0}, use_global_device_ids=true | all-gather | bytes 40960 | tf_op jit(solution)/shard_map/all_gather | solution.py:13
  101.0 15.8 %all-gather.15.cloned.1.call-done = bf16[4,512,512]{2,1,0:T(8,128)(2,1)} async-done(((bf16[1,512,512]{2,1,0:T(8,128)(2,1)}), bf16[4,512,512]{2,1,0:T(8,128)(2,1)}) %all-gather.15.cloned.1.call-update) | async-done | bytes 2097168 | tf_op jit(solution)/shard_map/all_gather | solution.py:13
  116.9 1.2 fusion.65
  118.4 5.7 %while.24 = (s32[]{:T(128)}, f32[512,512]{0,1:T(8,128)S(1)}, f32[512,8]{0,1:T(8,128)S(1)}, f32[512,8]{0,1:T(8,128)S(1)}, bf16[4,512,8]{1,2,0:T(8,128)(2,1)S(1)},...) while((s32[]{:T(128)}, f32[512,512]{0,1:T(8,128)S(1)}, ...), condition=%wide.region_3.4_spmd, body=%wide.region_2.3_spmd.sunk | while | flops 1081349 | bytes 4866191 | solution.py:21
  118.4 1.1 constant_dynamic-slice_fusion.4
  119.7 0.5 fusion.139
  120.3 1.1 constant_dynamic-slice_fusion.4
  122.2 1.1 constant_dynamic-slice_fusion.4
  124.2 1.4 fusion.117
  125.8 2.2 fusion.118
  128.2 1.8 convolution_convert_fusion
  130.1 0.7 fusion.113
  131.5 12.4 %all_gather.49 = bf16[512,512]{1,0:T(8,128)(2,1)S(1)} all-gather(bf16[128,512]{1,0:T(8,128)(2,1)S(1)} %get-tuple-element.462), channel_id=1, replica_groups=mesh['row'=4,'col'=8] {'row'}, dimensions={0}, use_global_device_ids=true | all-gather | bytes 655360 | tf_op jit(solution)/shard_map/all_gather | solution.py:103
  144.1 9.6 %all-gather.19.cloned.1.call-done = bf16[1024,512]{1,0:T(8,128)(2,1)} async-done(((bf16[128,512]{1,0:T(8,128)(2,1)}), bf16[1024,512]{1,0:T(8,128)(2,1)}) %all-gather.19.cloned.1.call-update) | async-done | bytes 1048592 | tf_op jit(solution)/shard_map/all_gather | solution.py:100
  153.7 1.5 copy.39
  155.2 7.4 %select_reduce_fusion = (f32[8,512]{1,0:T(8,128)S(1)}, f32[8,512,1024]{2,1,0:T(8,128)}) fusion(pred[512,1024]{1,0:T(8,128)(4,1)S(1)} %bitcast.175, bf16[512,8,64]{0,2,1:T(8,128)(2,1)S(1)} %bitcast.181, bf16[1024,8,64]{0,2,1:T(8,128)(2,1)S(1)} %bitcast.179), kind=kOutput, calls=%fused_computation.23 | convolution fusion | flops 549449728 | bytes 18890752 | tf_op jit(solution)/shard_map/while/body/eval_jaxpr/qhd,khd->hqk/dot_general | solution.py:62
  162.6 16.2 %all-gather.17.cloned.1.call-done = bf16[1024,512]{1,0:T(8,128)(2,1)} async-done(((bf16[128,512]{1,0:T(8,128)(2,1)}), bf16[1024,512]{1,0:T(8,128)(2,1)}) %all-gather.17.cloned.1.call-update) | async-done | bytes 1048592 | tf_op jit(solution)/shard_map/all_gather | solution.py:101
  178.8 1.5 copy.37
  180.3 7.6 %fusion.23 = bf16[8,64,512]{2,1,0:T(8,128)(2,1)S(1)} fusion(bf16[1024,8,64]{0,2,1:T(8,128)(2,1)S(1)} %bitcast.184, f32[8,512,1024]{2,1,0:T(8,128)} %get-tuple-element.482, f32[8,512]{1,0:T(8,128)S(1)} %get-tuple-element.481, pred[512,1024]{1,0:T(8,128)(4,1)S(1)} %bitcast.176), kind=kOutput, calls=%fused_computation.42 | convolution fusion | flops 553910272 | bytes 18890752 | tf_op jit(solution)/shard_map/while/body/eval_jaxpr/hqk,khd->qhd/dot_general | solution.py:69
  187.9 1.0 copy.40
  189.0 8.2 %fusion.8 = bf16[8,512]{1,0:T(8,128)(2,1)S(1)} fusion(f32[8,512,1024]{2,1,0:T(8,128)} %get-tuple-element.482, f32[8,512]{1,0:T(8,128)S(1)} %get-tuple-element.481, pred[512,1024]{1,0:T(8,128)(4,1)S(1)} %bitcast.177), kind=kLoop, calls=%fused_computation.28 | loop fusion | flops 16773120 | bytes 17326080 | tf_op jit(solution)/shard_map/while/body/eval_jaxpr/reduce_sum | solution.py:68
  197.2 11.0 %all-gather.3 = bf16[2048,8]{0,1:T(8,128)(2,1)S(1)} all-gather(bf16[512,8]{0,1:T(8,128)(2,1)S(1)} %bitcast.192), channel_id=5, replica_groups=mesh['row'=4,'col'=8] {'row'}, dimensions={0}, use_global_device_ids=true | all-gather | bytes 40960 | tf_op jit(solution)/shard_map/all_gather | solution.py:13
  208.2 10.9 %all-gather.2 = bf16[2048,8]{0,1:T(8,128)(2,1)S(1)} all-gather(bf16[512,8]{0,1:T(8,128)(2,1)S(1)} %convert_bitcast_fusion.1), channel_id=4, replica_groups=mesh['row'=4,'col'=8] {'row'}, dimensions={0}, use_global_device_ids=true | all-gather | bytes 40960 | tf_op jit(solution)/shard_map/all_gather | solution.py:13
  219.1 16.2 %all-gather.21.cloned.1.call-done = bf16[4,512,512]{2,1,0:T(8,128)(2,1)} async-done(((bf16[1,512,512]{2,1,0:T(8,128)(2,1)}), bf16[4,512,512]{2,1,0:T(8,128)(2,1)}) %all-gather.21.cloned.1.call-update) | async-done | bytes 2097168 | tf_op jit(solution)/shard_map/all_gather | solution.py:13
  235.3 1.2 fusion.64
  236.8 5.7 %while.25 = (s32[]{:T(128)}, f32[512,512]{0,1:T(8,128)S(1)}, f32[512,8]{0,1:T(8,128)S(1)}, f32[512,8]{0,1:T(8,128)S(1)}, bf16[4,512,8]{1,2,0:T(8,128)(2,1)S(1)},...) while((s32[]{:T(128)}, f32[512,512]{0,1:T(8,128)S(1)}, ...), condition=%wide.region_11.12_spmd, body=%wide.region_10.11_spmd.sunk | while | flops 1081349 | bytes 4866191 | solution.py:21
  236.9 1.1 constant_dynamic-slice_fusion.5
  238.8 1.1 constant_dynamic-slice_fusion.5
  240.7 1.1 constant_dynamic-slice_fusion.5
  242.6 1.4 fusion.121
  244.2 2.2 fusion.122
  246.6 0.8 add_convert_fusion
  (78 shorter events, 7.7 us)
Async XLA Ops:
  6.5 3.5 %copy-start = (s32[32,32]{1,0:T(8,128)S(1)}, s32[32,32]{1,0:T(8,128)}, u32[]{:S(2)}) copy-start(s32[32,32]{1,0:T(8,128)} %param.13) | copy-start | bytes 12292
  6.5 28.6 %all-gather.13.cloned.1.call-start = ((), (), s32[]{:S(2)}) async-start(), calls=%async_computation.1 | async-start | bytes 1179648 | tf_op jit(solution)/shard_map/all_gather | solution.py:100
  9.2 51.3 %all-gather.11.cloned.1.call-start = ((), (), s32[]{:S(2)}) async-start(), calls=%async_computation | async-start | bytes 1179648 | tf_op jit(solution)/shard_map/all_gather | solution.py:101
  9.9 107.0 %all-gather.15.cloned.1.call-start = ((), (), s32[]{:S(2)}) async-start(), calls=%async_computation.2 | async-start | bytes 2621440 | tf_op jit(solution)/shard_map/all_gather | solution.py:13
  44.1 26.6 %copy-start.3 = (f32[2,2,512]{2,1,0:T(2,128)S(1)}, f32[2,2,512]{2,1,0:T(2,128)}, u32[]{:S(2)}) copy-start(f32[2,2,512]{2,1,0:T(2,128)} %param.18) | copy-start | bytes 24580
  44.1 26.6 %copy-start.4 = (f32[2,2,512]{2,1,0:T(2,128)S(1)}, f32[2,2,512]{2,1,0:T(2,128)}, u32[]{:S(2)}) copy-start(f32[2,2,512]{2,1,0:T(2,128)} %param.19) | copy-start | bytes 24580
  70.6 83.1 %all-gather.19.cloned.1.call-start = ((), (), s32[]{:S(2)}) async-start(), calls=%async_computation.4 | async-start | bytes 1179648 | tf_op jit(solution)/shard_map/all_gather | solution.py:100
  78.9 45.3 %copy-start.2 = (bf16[128,512]{1,0:T(8,128)(2,1)S(1)}, bf16[128,512]{1,0:T(8,128)(2,1)}, u32[]{:S(2)}) copy-start(bf16[128,512]{1,0:T(8,128)(2,1)} %param.12) | copy-start | bytes 393220
  130.8 48.0 %all-gather.17.cloned.1.call-start = ((), (), s32[]{:S(2)}) async-start(), calls=%async_computation.3 | async-start | bytes 1179648 | tf_op jit(solution)/shard_map/all_gather | solution.py:101
  131.4 103.9 %all-gather.21.cloned.1.call-start = ((), (), s32[]{:S(2)}) async-start(), calls=%async_computation.5 | async-start | bytes 2621440 | tf_op jit(solution)/shard_map/all_gather | solution.py:13
  235.3 12.1 %copy-start.1 = (s32[32,32]{1,0:T(8,128)S(1)}, s32[32,32]{1,0:T(8,128)}, u32[]{:S(2)}) copy-start(s32[32,32]{1,0:T(8,128)} %param.13) | copy-start | bytes 12292
Sparse Core Ops, SparseCore 0:
  9.3 25.8 all-gather.12
  37.0 23.3 all-gather.10
  70.7 46.1 all-gather.14
  131.0 22.7 all-gather.18
  155.4 23.3 all-gather.16
  189.1 46.1 all-gather.20
where the time goes:
time: 256 us; the launch traced here: 254 us
  waiting for transfers between devices  81.7 us (32%)
  blocking collectives  71.8 us (28%)
  matrix products  41 us (16%)
  other arithmetic  24.1 us (9%)
  local copies, waits for them, and re-layouts  21.5 us (8%)
  between operations  13.8 us (5%)
    all_gather x4, blocking collectives, combined_all(): lax.all_gather(part.astype(kind), axis)  44 us
    all_gather x2, waiting for transfers between devices, per_device(): lax.all_gather(pair[1], 'col', axis=0, tiled=True)  32.6 us
    all_gather x2, waiting for transfers between devices, combined_all(): lax.all_gather(part.astype(kind), axis)  32 us
    all_gather x2, blocking collectives, per_device(): queries = lax.all_gather(own_q, 'row', axis=0, tiled=True)  27.7 us
    reduce_sum x2, other arithmetic, one_block(): mass = jnp.sum(weights, axis=-1)  16.4 us
    all_gather x2, waiting for transfers between devices, per_device(): lax.all_gather(pair[0], 'col', axis=0, tiled=True)  15.8 us
    dot_general x2, matrix products, one_block(): jnp.einsum('hqk,khd->qhd', weights.astype(jnp.bfloat16), vsplit, preferre...  15.2 us
    dot_general x2, matrix products, one_block(): jnp.einsum('qhd,khd->hqk', qpart, ksplit, preferred_element_type=jnp.floa...  14.8 us
  transfers between devices with their start and end apart: 6, of which 6 were waited for; matrix products, arithmetic and copies ran while one was open for 15% of the time, Pallas kernels for 0%

commit v1 on v0

v1 whole, which is shorter than its diff:
```python
import functools

import jax
import jax.numpy as jnp
from jax import lax
from jax.experimental import pallas as pl
from jax.experimental.pallas import tpu as pltpu
from jax.sharding import PartitionSpec as P

HEADS = 8
BLOCK = 128
HALF = HEADS // 2
NEG = -1e30
BIG = 1e30
MESH = pl.DeviceIdType.MESH
F32 = jnp.float32
BF16 = jnp.bfloat16


def bits_of(n):
    return [1 << b for b in range(max(n - 1, 0).bit_length())]


def partner_of(i, k, n):
    out = i
    for b in bits_of(n):
        own = lax.rem(lax.div(i, b), 2)
        flip = (k // b) % 2 if isinstance(k, int) else lax.rem(lax.div(k, b), 2)
        out = out + b * (lax.rem(own + flip, 2) - own)
    return out


def layer_norm(values, gain, bias):
    center = values - jnp.mean(values, axis=-1, keepdims=True)
    spread = jnp.mean(center * center, axis=-1, keepdims=True)
    return center * lax.rsqrt(spread + 1e-05) * gain + bias


def kernel(
    n_row, chips, layers,
    x_ref, mask_ref, wqkv_hbm, wout_hbm, wup_hbm, wdown_hbm, gain_ref, bias_ref,
    out_ref,
    wqkv, wout, wup, wdown, wsem,
    xbuf, xs, qsend, qbuf, rs, st, obuf, sbuf,
    kbuf, vbuf, qpad, acc, top,
    xz_send, xz_recv, xd_send, xd_recv, q_send, q_recv, o_send, o_recv, s_send, s_recv,
):
    rows, width = x_ref.shape
    head_dim = width // HEADS
    hw = width // 2
    n_col = 2 * chips
    z = lax.axis_index("row")
    col = lax.axis_index("col")
    p = lax.div(col, 2)
    c = lax.rem(col, 2)
    mate = 2 * p + 1 - c

    def weight_copies(layer):
        pairs = ((wqkv_hbm, wqkv), (wout_hbm, wout), (wup_hbm, wup), (wdown_hbm, wdown))
        return [
            pltpu.make_async_copy(a.at[layer], b.at[layer], wsem.at[layer, i])
            for i, (a, b) in enumerate(pairs)
        ]

    for layer in range(layers):
        for copy in weight_copies(layer):
            copy.start()

    barrier = pltpu.get_barrier_semaphore()
    for k in range(1, n_row):
        pl.semaphore_signal(
            barrier, inc=1, device_id=(partner_of(z, k, n_row), col), device_id_type=MESH
        )
    pl.semaphore_signal(barrier, inc=1, device_id=(z, mate), device_id_type=MESH)
    for k in range(1, chips):
        for d in range(2):
            pl.semaphore_signal(
                barrier, inc=1, device_id=(z, 2 * partner_of(p, k, chips) + d), device_id_type=MESH
            )
    pl.semaphore_wait(barrier, n_row - 1 + 1 + 2 * (chips - 1))

    def send(src, dst, send_sem, recv_sem, row, column):
        return pltpu.make_async_remote_copy(
            src_ref=src, dst_ref=dst, send_sem=send_sem, recv_sem=recv_sem,
            device_id=(row, column), device_id_type=MESH,
        )

    lane = lax.broadcasted_iota(jnp.int32, (1, 2 * BLOCK), 1)
    ones = jnp.ones((16, 2 * BLOCK), BF16)
    pad = jnp.zeros((head_dim, 2 * BLOCK), BF16)

    for layer in range(layers):
        own_x = x_ref if layer == 0 else xs.at[layer]

        x_copies = [
            send(own_x, xbuf.at[layer, k, c], xz_send.at[layer, k], xz_recv.at[layer, k],
                 partner_of(z, k, n_row), col)
            for k in range(1, n_row)
        ]
        d_copies = [
            send(own_x if k == 0 else xbuf.at[layer, k, c], xbuf.at[layer, k, c],
                 xd_send.at[layer, k], xd_recv.at[layer, k], z, mate)
            for k in range(n_row)
        ]
        d_copies[0].start()
        for copy in x_copies:
            copy.start()
        x = own_x[...]
        xbuf[layer, 0, c] = x

        weight_copies(layer)[0].wait()
        q = jnp.dot(x, wqkv[layer, :, :width], preferred_element_type=F32)
        q = q.astype(BF16).astype(F32) * (1.0 / head_dim**0.5)
        qt = q.T.astype(BF16)
        for d in range(2):
            qsend[layer, d] = qt[d * hw:(d + 1) * hw]
        q_copies = []
        for k in range(1, chips):
            for d in range(2):
                q_copies.append(
                    send(qsend.at[layer, d], qbuf.at[layer, k, c],
                         q_send.at[layer, k, d], q_recv.at[layer, k, c],
                         z, 2 * partner_of(p, k, chips) + d)
                )
        q_copies.append(
            send(qsend.at[layer, 1 - c], qbuf.at[layer, 0, c],
                 q_send.at[layer, 0, 0], q_recv.at[layer, 0, c], z, mate)
        )
        for copy in q_copies[::-1]:
            copy.start()
        qbuf[layer, 0, c] = qsend[layer, c]

        def wait_q(m, j):
            send(qsend.at[layer, 0], qbuf.at[layer, m, j], q_send.at[layer, 0, 0],
                 q_recv.at[layer, m, j], z, mate).wait_recv()

        def o_copy(m, j, half, column):
            return (
                send(rs.at[layer, m, j], obuf.at[layer, m, half],
                     o_send.at[layer, m, j], o_recv.at[layer, m, half], z, column),
                send(st.at[layer, m, j], sbuf.at[layer, m, half],
                     s_send.at[layer, m, j], s_recv.at[layer, m, half], z, column),
            )

        def pair(step, m):
            first, last = step == 0, step == n_row - 1
            if first:
                for h in range(HALF):
                    block = jnp.concatenate(
                        [qbuf[layer, m, j, h * head_dim:(h + 1) * head_dim, :] for j in range(2)],
                        axis=1,
                    )
                    qpad[m, h] = jnp.concatenate(
                        [block, pad] if h % 2 == 0 else [pad, block], axis=0
                    )
            key_row = partner_of(z, step, n_row)
            q_chip = partner_of(p, m, chips)
            allowed = []
            for j in range(2):
                key_id = key_row * n_col + 2 * p + j
                query_id = z * n_col + 2 * q_chip
                near = mask_ref[query_id, key_id]
                far = mask_ref[query_id + 1, key_id]
                allowed.append(jnp.where(lane < BLOCK, near, far) > 0)
            for h in range(HALF):
                group = (h // 2) * 2 * head_dim
                s = jnp.dot(
                    kbuf[:, group:group + 2 * head_dim], qpad[m, h], preferred_element_type=F32
                )
                parts = [s[:BLOCK], s[BLOCK:]]
                peaks = [
                    jnp.where(ok, jnp.max(part, axis=0, keepdims=True), NEG)
                    for ok, part in zip(allowed, parts)
                ]
                peak = jnp.maximum(*peaks)
                if not first:
                    before = top[m, h:h + 1, :]
                    peak = jnp.maximum(peak, before)
                weights = jnp.concatenate(
                    [jnp.exp(part - jnp.where(ok, peak, BIG)) for ok, part in zip(allowed, parts)],
                    axis=0,
                ).astype(BF16)
                total = jnp.dot(vbuf[h], weights, preferred_element_type=F32)
                if not first:
                    total = total + acc[m, h] * jnp.exp(before - peak)
                if last:
                    mass = total[head_dim:head_dim + 1]
                    part = (total[:head_dim] / jnp.maximum(mass, 1e-30)).astype(BF16)
                    for j in range(2):
                        cut = slice(j * BLOCK, (j + 1) * BLOCK)
                        rs[layer, m, j, h * head_dim:(h + 1) * head_dim, :] = part[:, cut]
                        st[layer, m, j, h:h + 1, :] = peak[:, cut]
                        st[layer, m, j, HALF + h:HALF + h + 1, :] = mass[:, cut]
                else:
                    acc[m, h] = total
                    top[m, h:h + 1, :] = peak

        for step in range(n_row):
            if step > 0:
                x_copies[step - 1].wait_recv()
                d_copies[step].start()
            d_copies[step].wait_recv()
            chunk = xbuf[layer, step].reshape(2 * rows, width)
            k_cols = pl.ds(pl.multiple_of(width + c * hw, hw), hw)
            v_cols = pl.ds(pl.multiple_of(2 * width + c * hw, hw), hw)
            kbuf[...] = jnp.dot(
                chunk, wqkv[layer, :, k_cols], preferred_element_type=F32
            ).astype(BF16)
            vt = jnp.dot(chunk, wqkv[layer, :, v_cols], preferred_element_type=F32).T.astype(BF16)
            for h in range(HALF):
                vbuf[h] = jnp.concatenate([vt[h * head_dim:(h + 1) * head_dim], ones], axis=0)
            if step == 0:
                wait_q(0, 1 - c)
                pair(step, 0)

            def body(i, carry, step=step):
                m = i + 1 if step < n_row - 1 else chips - 1 - i
                if step == 0:
                    wait_q(m, 0)
                    wait_q(m, 1)
                pair(step, m)
                if step == n_row - 1:
                    for j in range(2):
                        for copy in o_copy(m, j, c, 2 * partner_of(p, m, chips) + j):
                            copy.start()
                return carry

            lax.fori_loop(0, chips - 1, body, 0)
            if step > 0:
                pair(step, 0)
        for copy in o_copy(0, 1 - c, c, mate):
            copy.start()
        obuf[layer, 0, c] = rs[layer, 0, c]
        sbuf[layer, 0, c] = st[layer, 0, c]

        for copy in weight_copies(layer)[1:]:
            copy.wait()
        for m in range(chips):
            for half in range(2):
                if m > 0:
                    for copy in o_copy(m, half, half, mate):
                        copy.wait_recv()
        for copy in o_copy(0, 1 - c, 1 - c, mate):
            copy.wait_recv()
        heads = []
        for half in range(2):
            for h in range(HALF):
                tops = [sbuf[layer, m, half, h:h + 1, :] for m in range(chips)]
                peak = functools.reduce(jnp.maximum, tops)
                scale = [
                    sbuf[layer, m, half, HALF + h:HALF + h + 1, :] * jnp.exp(tops[m] - peak)
                    for m in range(chips)
                ]
                inverse = 1.0 / functools.reduce(jnp.add, scale)
                cut = slice(h * head_dim, (h + 1) * head_dim)
                heads.append(
                    functools.reduce(
                        jnp.add,
                        [
                            obuf[layer, m, half, cut, :].astype(F32) * (scale[m] * inverse)
                            for m in range(chips)
                        ],
                    )
                )
        attn = jnp.concatenate(heads, axis=0).T.astype(BF16)

        mixed = jnp.dot(attn, wout[layer], preferred_element_type=F32)
        hidden = layer_norm(
            x.astype(F32) + mixed, gain_ref[layer, 0:1, :], bias_ref[layer, 0:1, :]
        ).astype(BF16)
        up = jax.nn.gelu(jnp.dot(hidden, wup[layer], preferred_element_type=F32)).astype(BF16)
        down = jnp.dot(up, wdown[layer], preferred_element_type=F32)
        result = layer_norm(
            hidden.astype(F32) + down, gain_ref[layer, 1:2, :], bias_ref[layer, 1:2, :]
        ).astype(BF16)
        if layer == layers - 1:
            out_ref[...] = result
        else:
            xs[layer + 1] = result

        for copy in x_copies + d_copies + q_copies:
            copy.wait_send()
        for m in range(chips):
            for j in range(2):
                if m > 0:
                    for copy in o_copy(m, j, c, mate):
                        copy.wait_send()
        for copy in o_copy(0, 1 - c, c, mate):
            copy.wait_send()


def per_device(n_row, n_col, node_feats, block_mask, w_qkv, w_out, w_up, w_down, ln_gain, ln_bias):
    rows, width = node_feats.shape
    layers = w_qkv.shape[0]
    chips = n_col // 2
    assert rows == BLOCK
    hw = width // 2
    head_dim = width // HEADS
    vmem = pl.BlockSpec(memory_space=pltpu.VMEM)
    hbm = pl.BlockSpec(memory_space=pl.ANY)
    dma = pltpu.SemaphoreType.DMA
    return pl.pallas_call(
        functools.partial(kernel, n_row, chips, layers),
        out_shape=jax.ShapeDtypeStruct((rows, width), BF16),
        in_specs=[vmem, pl.BlockSpec(memory_space=pltpu.SMEM), hbm, hbm, hbm, hbm, vmem, vmem],
        out_specs=vmem,
        scratch_shapes=[
            pltpu.VMEM(w_qkv.shape, BF16),
            pltpu.VMEM(w_out.shape, BF16),
            pltpu.VMEM(w_up.shape, BF16),
            pltpu.VMEM(w_down.shape, BF16),
            dma((layers, 4)),
            pltpu.VMEM((layers, n_row, 2, rows, width), BF16),
            pltpu.VMEM((layers, rows, width), BF16),
            pltpu.VMEM((layers, 2, hw, rows), BF16),
            pltpu.VMEM((layers, chips, 2, hw, rows), BF16),
            pltpu.VMEM((layers, chips, 2, hw, rows), BF16),
            pltpu.VMEM((layers, chips, 2, HEADS, rows), F32),
            pltpu.VMEM((layers, chips, 2, hw, rows), BF16),
            pltpu.VMEM((layers, chips, 2, HEADS, rows), F32),
            pltpu.VMEM((2 * rows, hw), BF16),
            pltpu.VMEM((HALF, head_dim + 16, 2 * rows), BF16),
            pltpu.VMEM((chips, HALF, 2 * head_dim, 2 * rows), BF16),
            pltpu.VMEM((chips, HALF, head_dim + 16, 2 * rows), F32),
            pltpu.VMEM((chips, HEADS, 2 * rows), F32),
            dma((layers, n_row)),
            dma((layers, n_row)),
            dma((layers, n_row)),
            dma((layers, n_row)),
            dma((layers, chips, 2)),
            dma((layers, chips, 2)),
            dma((layers, chips, 2)),
            dma((layers, chips, 2)),
            dma((layers, chips, 2)),
            dma((layers, chips, 2)),
        ],
        compiler_params=pltpu.CompilerParams(
            collective_id=0, has_side_effects=True, vmem_limit_bytes=56 * 1024 * 1024
        ),
    )(node_feats, block_mask, w_qkv, w_out, w_up, w_down, ln_gain, ln_bias)


def solution(mesh):
    placed = (P(("row", "col"), None), P(), P(), P(), P(), P(), P(), P())
    body = functools.partial(per_device, mesh.shape["row"], mesh.shape["col"])
    return jax.shard_map(
        body, mesh=mesh, in_specs=placed, out_specs=P(("row", "col"), None), check_vma=False
    )
```

time: 256 us -> 79.3 us (0.31)
  waiting for transfers between devices: 81.7 us -> 0 us
  Pallas kernels: 0 us -> 77.5 us
  blocking collectives: 71.8 us -> 0 us
  matrix products: 41 us -> 0 us
  other arithmetic: 24.1 us -> 0 us
  local copies, waits for them, and re-layouts: 21.5 us -> 1.57 us
  between operations: 13.8 us -> 0.01 us
    all_gather x6 -> x0, waiting for transfers between devices: 80.4 us -> none  [the longest x2 32.6 us: per_device(): lax.all_gather(pair[1], 'col', axis=0, tiled=True)]
    pallas_call x0 -> x1, Pallas kernels: none -> 77.5 us  [per_device(): pl.pallas_call(functools.partial(kernel, n_row, chips, layers), out_shape...]
    all_gather x6 -> x0, blocking collectives: 71.8 us -> none  [the longest x4 44 us: combined_all(): lax.all_gather(part.astype(kind), axis)]
    dot_general x10 -> x0, matrix products: 41 us -> none  [the longest x2 15.2 us: one_block(): jnp.einsum('hqk,khd->qhd', weights.astype(jnp.bfloat16), vsplit, preferre...]
    reduce_sum x6 -> x0, other arithmetic: 17.1 us -> none  [the longest x2 16.4 us: one_block(): mass = jnp.sum(weights, axis=-1)]
    dynamic_slice x12 -> x0, local copies, waits for them, and re-layouts: 7.77 us -> none  [take(): part[k].astype(own.dtype)]
    all_gather x6 -> x0, local copies, waits for them, and re-layouts: 6.35 us -> none  [the longest x2 2.96 us: per_device(): lax.all_gather(pair[1], 'col', axis=0, tiled=True)]
    add x12 -> x0, other arithmetic: 3.42 us -> none  [the longest x6 3.28 us: combine(): per_head(sum_a, scale_a) + per_head(sum_b, scale_b)]
  transfers between devices with their start and end apart: 6 -> 0, of which waited for: 6 -> 0; matrix products, arithmetic and copies ran while one was open for 15% -> 0% of each run, Pallas kernels for 0% -> 0%
where the time goes in v1:
time: 79.3 us; the launch traced here: 79.1 us
  Pallas kernels  77.5 us (98%)
  local copies, waits for them, and re-layouts  1.57 us (2%)
    pallas_call x1, Pallas kernels, per_device(): pl.pallas_call(functools.partial(kernel, n_row, chips, layers), out_shape...  77.5 us

profile of v1, /device:TPU:1, one launch (start us, length us, event | category | flops | bytes accessed | tf_op | source)
XLA Modules:
  0.0 79.1 jit_solution(595857823125677720)
XLA Ops:
  0.0 77.5 %shard_map.82 = bf16[128,512]{1,0:T(8,128)(2,1)} custom-call(bf16[128,512]{1,0:T(8,128)(2,1)} %x_ref.1, s32[32,32]{1,0:T(8,128)} %mask_ref.1, bf16[2,512,1536]{2,1,0:T(8,128)(2,1)} %wqkv_hbm.1, bf16[2,512,512]{2,1,0:T(8,128)(2,1)} %wout_hbm.1, bf16[2,512,1024]{2,1,0:T(8,128)(2,1)} %wup_hbm.1, bf16[2,1024,512]{2,1,0:T(8,128)(2,1)} %wdown_hbm.1, ...), custom_call_target="tpu_custom_call" | custom-call | tf_op jit(solution)/shard_map/pallas_call | solution.py:302
  77.5 1.6 %copy.10 = bf16[128,512]{1,0:T(8,128)(2,1)} copy(bf16[128,512]{1,0:T(8,128)(2,1)} %shard_map.82) | data formatting | bytes 262144

commit v2 on v1

--- a/solution.py
+++ b/solution.py
@@ -10,6 +10,7 @@
 HEADS = 8
 BLOCK = 128
 HALF = HEADS // 2
+KEEP = 1
 NEG = -1e30
 BIG = 1e30
 MESH = pl.DeviceIdType.MESH
@@ -85,6 +86,8 @@
             device_id=(row, column), device_id_type=MESH,
         )
 
+    order = list(range(n_row))
+
     lane = lax.broadcasted_iota(jnp.int32, (1, 2 * BLOCK), 1)
     ones = jnp.ones((16, 2 * BLOCK), BF16)
     pad = jnp.zeros((head_dim, 2 * BLOCK), BF16)
@@ -92,19 +95,19 @@
     for layer in range(layers):
         own_x = x_ref if layer == 0 else xs.at[layer]
 
-        x_copies = [
-            send(own_x, xbuf.at[layer, k, c], xz_send.at[layer, k], xz_recv.at[layer, k],
-                 partner_of(z, k, n_row), col)
-            for k in range(1, n_row)
-        ]
+        x_copies = {
+            k: send(own_x, xbuf.at[layer, k, c], xz_send.at[layer, k], xz_recv.at[layer, k],
+                    partner_of(z, k, n_row), col)
+            for k in order[1:]
+        }
         d_copies = [
             send(own_x if k == 0 else xbuf.at[layer, k, c], xbuf.at[layer, k, c],
                  xd_send.at[layer, k], xd_recv.at[layer, k], z, mate)
             for k in range(n_row)
         ]
         d_copies[0].start()
-        for copy in x_copies:
-            copy.start()
+        for k in order[1:]:
+            x_copies[k].start()
         x = own_x[...]
         xbuf[layer, 0, c] = x
 
@@ -143,7 +146,7 @@
             )
 
         def pair(step, m):
-            first, last = step == 0, step == n_row - 1
+            first, last = step == order[0], step == order[-1]
             if first:
                 for h in range(HALF):
                     block = jnp.concatenate(
@@ -162,27 +165,34 @@
                 near = mask_ref[query_id, key_id]
                 far = mask_ref[query_id + 1, key_id]
                 allowed.append(jnp.where(lane < BLOCK, near, far) > 0)
+            scores, peaks, before = [], [], []
             for h in range(HALF):
                 group = (h // 2) * 2 * head_dim
-                s = jnp.dot(
+                scores.append(jnp.dot(
                     kbuf[:, group:group + 2 * head_dim], qpad[m, h], preferred_element_type=F32
-                )
-                parts = [s[:BLOCK], s[BLOCK:]]
-                peaks = [
+                ))
+            weights = []
+            for h in range(HALF):
+                parts = [scores[h][:BLOCK], scores[h][BLOCK:]]
+                peak = jnp.maximum(*[
                     jnp.where(ok, jnp.max(part, axis=0, keepdims=True), NEG)
                     for ok, part in zip(allowed, parts)
-                ]
-                peak = jnp.maximum(*peaks)
+                ])
                 if not first:
-                    before = top[m, h:h + 1, :]
-                    peak = jnp.maximum(peak, before)
-                weights = jnp.concatenate(
+                    before.append(top[m, h:h + 1, :])
+                    peak = jnp.maximum(peak, before[h])
+                peaks.append(peak)
+                weights.append(jnp.concatenate(
                     [jnp.exp(part - jnp.where(ok, peak, BIG)) for ok, part in zip(allowed, parts)],
                     axis=0,
-                ).astype(BF16)
-                total = jnp.dot(vbuf[h], weights, preferred_element_type=F32)
+                ).astype(BF16))
+            totals = [
+                jnp.dot(vbuf[h], weights[h], preferred_element_type=F32) for h in range(HALF)
+            ]
+            for h in range(HALF):
+                total, peak = totals[h], peaks[h]
                 if not first:
-                    total = total + acc[m, h] * jnp.exp(before - peak)
+                    total = total + acc[m, h] * jnp.exp(before[h] - peak)
                 if last:
                     mass = total[head_dim:head_dim + 1]
                     part = (total[:head_dim] / jnp.maximum(mass, 1e-30)).astype(BF16)
@@ -195,10 +205,12 @@
                     acc[m, h] = total
                     top[m, h:h + 1, :] = peak
 
-        for step in range(n_row):
-            if step > 0:
-                x_copies[step - 1].wait_recv()
-                d_copies[step].start()
+        def pass_on(step):
+            x_copies[step].wait_recv()
+            d_copies[step].start()
+
+        for turn, step in enumerate(order):
+            final = turn == n_row - 1
             d_copies[step].wait_recv()
             chunk = xbuf[layer, step].reshape(2 * rows, width)
             k_cols = pl.ds(pl.multiple_of(width + c * hw, hw), hw)
@@ -209,24 +221,28 @@
             vt = jnp.dot(chunk, wqkv[layer, :, v_cols], preferred_element_type=F32).T.astype(BF16)
             for h in range(HALF):
                 vbuf[h] = jnp.concatenate([vt[h * head_dim:(h + 1) * head_dim], ones], axis=0)
-            if step == 0:
+            if turn == 0:
                 wait_q(0, 1 - c)
                 pair(step, 0)
 
-            def body(i, carry, step=step):
-                m = i + 1 if step < n_row - 1 else chips - 1 - i
-                if step == 0:
+            def body(i, carry, turn=turn, step=step, final=final):
+                m = chips - 1 - i if final else i + 1
+                if turn == 0:
                     wait_q(m, 0)
                     wait_q(m, 1)
                 pair(step, m)
-                if step == n_row - 1:
+                if final:
                     for j in range(2):
                         for copy in o_copy(m, j, c, 2 * partner_of(p, m, chips) + j):
                             copy.start()
                 return carry
 
-            lax.fori_loop(0, chips - 1, body, 0)
-            if step > 0:
+            early = chips - 1 if final else max(chips - 1 - KEEP, 0)
+            lax.fori_loop(0, early, body, 0)
+            if not final:
+                pass_on(order[turn + 1])
+                lax.fori_loop(early, chips - 1, body, 0)
+            if turn > 0:
                 pair(step, 0)
         for copy in o_copy(0, 1 - c, c, mate):
             copy.start()
@@ -278,7 +294,9 @@
         else:
             xs[layer + 1] = result
 
-        for copy in x_copies + d_copies + q_copies:
+        for k in order[1:]:
+            x_copies[k].wait_send()
+        for copy in d_copies + q_copies:
             copy.wait_send()
         for m in range(chips):
             for j in range(2):

time: 79.3 us -> 60.1 us (0.76)
  Pallas kernels: 77.5 us -> 58.4 us
    pallas_call x1, Pallas kernels: 77.5 us -> 58.4 us  [per_device(): pl.pallas_call(functools.partial(kernel, n_row, chips, layers), out_shape...]
where the time goes in v2:
time: 60.1 us; the launch traced here: 60 us
  Pallas kernels  58.4 us (97%)
  local copies, waits for them, and re-layouts  1.57 us (3%)
    pallas_call x1, Pallas kernels, per_device(): pl.pallas_call(functools.partial(kernel, n_row, chips, layers), out_shape...  58.4 us
    unnamed x1, local copies, waits for them, and re-layouts  1.57 us

profile of v2, /device:TPU:1, one launch (start us, length us, event | category | flops | bytes accessed | tf_op | source)
XLA Modules:
  0.0 60.0 jit_solution(4326524388817522949)
XLA Ops:
  0.0 58.4 %shard_map.82 = bf16[128,512]{1,0:T(8,128)(2,1)} custom-call(bf16[128,512]{1,0:T(8,128)(2,1)} %x_ref.1, s32[32,32]{1,0:T(8,128)} %mask_ref.1, bf16[2,512,1536]{2,1,0:T(8,128)(2,1)} %wqkv_hbm.1, bf16[2,512,512]{2,1,0:T(8,128)(2,1)} %wout_hbm.1, bf16[2,512,1024]{2,1,0:T(8,128)(2,1)} %wup_hbm.1, bf16[2,1024,512]{2,1,0:T(8,128)(2,1)} %wdown_hbm.1, ...), custom_call_target="tpu_custom_call" | custom-call | tf_op jit(solution)/shard_map/pallas_call | solution.py:320
  58.4 1.6 %copy.10 = bf16[128,512]{1,0:T(8,128)(2,1)} copy(bf16[128,512]{1,0:T(8,128)(2,1)} %shard_map.82) | data formatting | bytes 262144

commit v3 on v2

--- a/solution.py
+++ b/solution.py
@@ -129,7 +129,7 @@
             send(qsend.at[layer, 1 - c], qbuf.at[layer, 0, c],
                  q_send.at[layer, 0, 0], q_recv.at[layer, 0, c], z, mate)
         )
-        for copy in q_copies[::-1]:
+        for copy in q_copies[-1:] + q_copies[:-1]:
             copy.start()
         qbuf[layer, 0, c] = qsend[layer, c]
 
@@ -169,7 +169,7 @@
             for h in range(HALF):
                 group = (h // 2) * 2 * head_dim
                 scores.append(jnp.dot(
-                    kbuf[:, group:group + 2 * head_dim], qpad[m, h], preferred_element_type=F32
+                    kbuf[step, :, group:group + 2 * head_dim], qpad[m, h], preferred_element_type=F32
                 ))
             weights = []
             for h in range(HALF):
@@ -187,7 +187,7 @@
                     axis=0,
                 ).astype(BF16))
             totals = [
-                jnp.dot(vbuf[h], weights[h], preferred_element_type=F32) for h in range(HALF)
+                jnp.dot(vbuf[step, h], weights[h], preferred_element_type=F32) for h in range(HALF)
             ]
             for h in range(HALF):
                 total, peak = totals[h], peaks[h]
@@ -209,28 +209,39 @@
             x_copies[step].wait_recv()
             d_copies[step].start()
 
-        for turn, step in enumerate(order):
-            final = turn == n_row - 1
-            d_copies[step].wait_recv()
+        def project(step):
             chunk = xbuf[layer, step].reshape(2 * rows, width)
             k_cols = pl.ds(pl.multiple_of(width + c * hw, hw), hw)
             v_cols = pl.ds(pl.multiple_of(2 * width + c * hw, hw), hw)
-            kbuf[...] = jnp.dot(
+            kbuf[step] = jnp.dot(
                 chunk, wqkv[layer, :, k_cols], preferred_element_type=F32
             ).astype(BF16)
             vt = jnp.dot(chunk, wqkv[layer, :, v_cols], preferred_element_type=F32).T.astype(BF16)
             for h in range(HALF):
-                vbuf[h] = jnp.concatenate([vt[h * head_dim:(h + 1) * head_dim], ones], axis=0)
+                vbuf[step, h] = jnp.concatenate(
+                    [vt[h * head_dim:(h + 1) * head_dim], ones], axis=0
+                )
+
+        d_copies[order[0]].wait_recv()
+        project(order[0])
+        wait_q(0, 1 - c)
+        pair(order[0], 0)
+        groups = [order[:2]] + [[step] for step in order[2:]]
+        pass_on(order[1])
+        for turn, group in enumerate(groups):
+            final = turn == len(groups) - 1
+            d_copies[group[-1]].wait_recv()
+            project(group[-1])
             if turn == 0:
-                wait_q(0, 1 - c)
-                pair(step, 0)
-
-            def body(i, carry, turn=turn, step=step, final=final):
+                pair(group[-1], 0)
+
+            def body(i, carry, turn=turn, group=group, final=final):
                 m = chips - 1 - i if final else i + 1
                 if turn == 0:
                     wait_q(m, 0)
                     wait_q(m, 1)
-                pair(step, m)
+                for step in group:
+                    pair(step, m)
                 if final:
                     for j in range(2):
                         for copy in o_copy(m, j, c, 2 * partner_of(p, m, chips) + j):
@@ -240,10 +251,10 @@
             early = chips - 1 if final else max(chips - 1 - KEEP, 0)
             lax.fori_loop(0, early, body, 0)
             if not final:
-                pass_on(order[turn + 1])
+                pass_on(groups[turn + 1][0])
                 lax.fori_loop(early, chips - 1, body, 0)
             if turn > 0:
-                pair(step, 0)
+                pair(group[0], 0)
         for copy in o_copy(0, 1 - c, c, mate):
             copy.start()
         obuf[layer, 0, c] = rs[layer, 0, c]
@@ -336,8 +347,8 @@
             pltpu.VMEM((layers, chips, 2, HEADS, rows), F32),
             pltpu.VMEM((layers, chips, 2, hw, rows), BF16),
             pltpu.VMEM((layers, chips, 2, HEADS, rows), F32),
-            pltpu.VMEM((2 * rows, hw), BF16),
-            pltpu.VMEM((HALF, head_dim + 16, 2 * rows), BF16),
+            pltpu.VMEM((n_row, 2 * rows, hw), BF16),
+            pltpu.VMEM((n_row, HALF, head_dim + 16, 2 * rows), BF16),
             pltpu.VMEM((chips, HALF, 2 * head_dim, 2 * rows), BF16),
             pltpu.VMEM((chips, HALF, head_dim + 16, 2 * rows), F32),
             pltpu.VMEM((chips, HEADS, 2 * rows), F32),

time: 60.1 us -> 58.5 us (0.973)
  Pallas kernels: 58.4 us -> 56.8 us
    pallas_call x1, Pallas kernels: 58.4 us -> 56.8 us  [per_device(): pl.pallas_call(functools.partial(kernel, n_row, chips, layers), out_shape...]
where the time goes in v3:
time: 58.5 us; the launch traced here: 58.4 us
  Pallas kernels  56.8 us (97%)
  local copies, waits for them, and re-layouts  1.57 us (3%)
    pallas_call x1, Pallas kernels, per_device(): pl.pallas_call(functools.partial(kernel, n_row, chips, layers), out_shape...  56.8 us
    unnamed x1, local copies, waits for them, and re-layouts  1.57 us

profile of v3, /device:TPU:1, one launch (start us, length us, event | category | flops | bytes accessed | tf_op | source)
XLA Modules:
  0.0 58.4 jit_solution(17228406295322799028)
XLA Ops:
  0.0 56.8 %shard_map.82 = bf16[128,512]{1,0:T(8,128)(2,1)} custom-call(bf16[128,512]{1,0:T(8,128)(2,1)} %x_ref.1, s32[32,32]{1,0:T(8,128)} %mask_ref.1, bf16[2,512,1536]{2,1,0:T(8,128)(2,1)} %wqkv_hbm.1, bf16[2,512,512]{2,1,0:T(8,128)(2,1)} %wout_hbm.1, bf16[2,512,1024]{2,1,0:T(8,128)(2,1)} %wup_hbm.1, bf16[2,1024,512]{2,1,0:T(8,128)(2,1)} %wdown_hbm.1, ...), custom_call_target="tpu_custom_call" | custom-call | tf_op jit(solution)/shard_map/pallas_call | solution.py:331
  56.8 1.6 %copy.10 = bf16[128,512]{1,0:T(8,128)(2,1)} copy(bf16[128,512]{1,0:T(8,128)(2,1)} %shard_map.82) | data formatting | bytes 262144
